TPU v7x, 32 devices: a whole 2x2x4 slice. The times are simulated.
32 devices in a mesh: scen: 8 (over z, x), rootr: 2 (over core), rootc: 2 (over y).
Axes of the slice: x: 2, y: 2, z: 4, core: 2. Of those that a mesh axis runs over, the one named last changes fastest.
Arguments:
- start_guess: float32 [8192, 256], P(('scen', 'rootr'), 'rootc'), may hold values from -6 to 6
- right_side: float32 [8192, 256], P(('scen', 'rootr'), 'rootc'), may hold values from -6 to 6
- root_diagonal: float32 [8192], P(('scen', 'rootr')), may hold values from 1 to 4
- preconditioner: bfloat16 [8192, 8192], P(('scen', 'rootr')), may hold values from -0.015625 to 0.015625
- border_block: bfloat16 [16, 512, 768], P(('scen', 'rootr'), 'rootc'), may hold values from -0.21875 to 0.21875
- coupling_inverse: bfloat16 [16, 512, 512], P(('scen', 'rootr'), 'rootc'), may hold values from -0.25 to 0.25
- border_count: int32 [16], P(('scen', 'rootr')), may hold values from 64 to 512, as said below
- column_tiles: int32 [16, 6], P(('scen', 'rootr')), may hold values from 0 to 63, as said below
Outputs:
- final_iterate: float32 [8192, 256], P(('scen', 'rootr'), 'rootc')
Inputs may be any that keep to these rules, and one draw needn't show every extreme that they name: A scenario's live border rows are its first border_count rows; some scenario has exactly 512. `column_tiles`: each row names 6 different tiles in rising order.
All inputs are finite; a program needn't handle non-finite values.
Results may differ from a plain program's by a relative error of at most 0.0022.
Values may be sent and summed in bfloat16 or wider, within the bound.
A program may use at most 64 MiB of HBM per device.

v0:
```python
import functools
import math

import jax
import jax.numpy as jnp
from jax import lax
from jax.experimental import pallas as pl
from jax.experimental.pallas import tpu as pltpu
from jax.sharding import PartitionSpec as P

TILE = 128
CHUNKS = 2
MESH = pl.DeviceIdType.MESH


class Gather:
    def __init__(self, place, buf, rows, sems):
        chunks = min(CHUNKS, rows)
        self.place, self.buf, self.chunks = place, buf, chunks
        self.step = rows // chunks
        self.rows = rows
        self.ring_send, self.ring_recv, self.pair_send, self.pair_recv = sems
        self.sent = []

    def piece(self, scen, core, chunk):
        first = (scen * 2 + core) * self.rows + chunk * self.step
        return self.buf.at[pl.ds(first, self.step)]

    def slot(self, way, hop, chunk):
        return (way * (self.place.hops + 1) + hop) * self.chunks + chunk

    def carried(self, way, hop):
        if hop < self.place.hops:
            return range(self.chunks)
        return [way] if way < self.chunks else []

    def ring_copy(self, way, hop, chunk, scen):
        at = self.slot(way, hop, chunk)
        ref = self.piece(scen, self.place.core, chunk)
        return pltpu.make_async_remote_copy(
            src_ref=ref,
            dst_ref=ref,
            send_sem=self.ring_send.at[at],
            recv_sem=self.ring_recv.at[at],
            device_id={"scen": self.place.ahead[way]},
            device_id_type=MESH,
        )

    def pair_copy(self, way, hop, chunk, scen, core):
        at = self.slot(way, hop, chunk)
        ref = self.piece(scen, core, chunk)
        return pltpu.make_async_remote_copy(
            src_ref=ref,
            dst_ref=ref,
            send_sem=self.pair_send.at[at],
            recv_sem=self.pair_recv.at[at],
            device_id={"rootr": 1 - self.place.core},
            device_id_type=MESH,
        )

    def send(self, copy):
        copy.start()
        self.sent.append(copy)

    def begin(self):
        for chunk in range(self.chunks):
            for way in range(2):
                if chunk in self.carried(way, 1):
                    self.send(self.ring_copy(way, 1, chunk, self.place.scen))
        for chunk in range(self.chunks):
            self.send(self.pair_copy(0, 0, chunk, self.place.scen, self.place.core))

    def advance(self, hop):
        for chunk in range(self.chunks):
            for way in range(2):
                if chunk not in self.carried(way, hop):
                    continue
                scen = self.place.origin(way, hop)
                self.ring_copy(way, hop, chunk, scen).wait_recv()
                if hop < self.place.hops and chunk in self.carried(way, hop + 1):
                    self.send(self.ring_copy(way, hop + 1, chunk, scen))
                self.send(self.pair_copy(way, hop, chunk, scen, self.place.core))

    def settle(self, hop):
        for chunk in range(self.chunks):
            for way in range(2):
                if hop == 0:
                    if way == 0:
                        self.pair_copy(0, 0, chunk, self.place.scen, 1 - self.place.core).wait_recv()
                elif chunk in self.carried(way, hop):
                    scen = self.place.origin(way, hop)
                    self.pair_copy(way, hop, chunk, scen, 1 - self.place.core).wait_recv()

    def finish(self):
        for copy in self.sent:
            copy.wait_send()


class Place:
    def __init__(self, count):
        self.count, self.hops = count, count // 2
        self.scen, self.core = lax.axis_index("scen"), lax.axis_index("rootr")
        side, level = lax.rem(self.scen, 2), lax.div(self.scen, 2)
        self.spot = level * (1 - side) + (count - 1 - level) * side
        self.ahead = [self.at(1), self.at(count - 1)]

    def at(self, shift):
        spot = lax.rem(self.spot + shift, self.count)
        upper = lax.div(spot, self.hops)
        return (1 - upper) * 2 * spot + upper * (2 * (self.count - 1 - spot) + 1)

    def origin(self, way, hop):
        return self.at(self.count - hop if way == 0 else hop)

    def origin_traced(self, way, hop):
        return self.at(self.count - hop + way * (2 * hop - self.count))


def kernel(
    count,
    guess_ref,
    right_ref,
    diagonal_ref,
    precon_hbm,
    border_hbm,
    inverse_hbm,
    live_ref,
    own_tiles_ref,
    tiles_row_ref,
    out_ref,
    low_all,
    own_all,
    term_all,
    tiles_all,
    tiles_smem,
    precon,
    border,
    inverse,
    local_sems,
    precon_sems,
    cross_send,
    cross_recv,
    *ring_sems,
):
    place = Place(count)
    side = lax.axis_index("rootc")
    own_rows, half_rhs = guess_ref.shape
    half_rows, coupled = border_hbm.shape[1:]
    touched = coupled // TILE
    own_block = place.scen * 2 + place.core

    own_half = pl.ds(pl.multiple_of(side * half_rows, half_rows), half_rows)
    other_half = pl.ds(pl.multiple_of((1 - side) * half_rows, half_rows), half_rows)
    load_border = pltpu.make_async_copy(border_hbm.at[0], border.at[own_half], local_sems.at[0])
    load_inverse = pltpu.make_async_copy(inverse_hbm.at[0], inverse.at[own_half], local_sems.at[1])
    columns_count = precon.shape[0]

    def load_column(t):
        columns = pl.ds(pl.multiple_of(t * TILE, TILE), TILE)
        return pltpu.make_async_copy(precon_hbm.at[:, columns], precon.at[t], precon_sems.at[t])

    load_border.start()
    load_inverse.start()

    unit = low_all.shape[1]
    units = own_rows // unit
    per_tile = TILE // unit
    own_slice = pl.ds(own_block * units, units)
    split = (units, unit, half_rhs)
    low_all[own_slice] = guess_ref[...].astype(jnp.bfloat16).reshape(split)
    scale = jnp.broadcast_to(diagonal_ref[...], (half_rhs, own_rows)).T
    own_terms = right_ref[...] - scale * guess_ref[...]
    own_all[own_slice] = own_terms.astype(jnp.bfloat16).reshape(split)
    tiles_all[pl.ds(own_block, 1)] = tiles_row_ref[...]

    barrier = pltpu.get_barrier_semaphore()
    for peer in (
        {"scen": place.ahead[0]},
        {"scen": place.ahead[1]},
        {"rootr": 1 - place.core},
        {"rootc": 1 - side},
    ):
        pl.semaphore_signal(barrier, inc=1, device_id=peer, device_id_type=MESH)
    pl.semaphore_wait(barrier, 4)

    low = Gather(place, low_all, units, ring_sems[0:4])
    own = Gather(place, own_all, units, ring_sems[4:8])
    term = Gather(place, term_all, touched, ring_sems[8:12])
    tiles = Gather(place, tiles_all, 1, ring_sems[12:16])

    crossings = []
    low.begin()
    for index, (source, target) in enumerate(((border_hbm, border), (inverse_hbm, inverse))):
        crossing = pltpu.make_async_remote_copy(
            src_ref=source.at[0],
            dst_ref=target.at[own_half],
            send_sem=cross_send.at[index],
            recv_sem=cross_recv.at[index],
            device_id={"rootc": 1 - side},
            device_id_type=MESH,
        )
        crossing.start()
        crossings.append(crossing)
    tiles.begin()

    @pl.loop(0, columns_count)
    def start_column(t):
        load_column(t).start()

    for hop in range(1, place.hops + 1):
        low.advance(hop)
        tiles.advance(hop)
    own.begin()
    for hop in range(place.hops + 1):
        low.settle(hop)

    load_border.wait()
    crossings[0].wait_recv()
    live = jnp.clip(live_ref[0], 0, 2 * half_rows)
    live_mask = lax.broadcasted_iota(jnp.int32, (2 * half_rows, half_rhs), 0) < live
    picked = jnp.concatenate(
        [
            low_all[own_tiles_ref[0, k] * per_tile + part]
            for k in range(touched)
            for part in range(per_tile)
        ],
        axis=0,
    )
    values = jnp.dot(border[...], picked, preferred_element_type=jnp.float32)
    values = jnp.where(live_mask, values, 0.0).astype(jnp.bfloat16)
    load_inverse.wait()
    crossings[1].wait_recv()
    solved = jnp.dot(inverse[...], values, preferred_element_type=jnp.float32)
    solved = jnp.where(live_mask, solved, 0.0).astype(jnp.bfloat16)
    terms = lax.dot_general(
        border[...], solved, (((0,), (0,)), ((), ())), preferred_element_type=jnp.float32
    )
    term_all[pl.ds(own_block * touched, touched)] = terms.astype(jnp.bfloat16).reshape(
        touched, TILE, half_rhs
    )
    term.begin()

    for hop in range(place.hops + 1):
        tiles.settle(hop)
    to_smem = pltpu.make_async_copy(tiles_all, tiles_smem, local_sems.at[3])
    to_smem.start()
    to_smem.wait()

    @pl.loop(0, columns_count)
    def wait_column(t):
        load_column(t).wait()

    out_ref[...] = guess_ref[...]

    def product(columns, values, rows):
        left = jnp.concatenate([precon[t] for t in columns], axis=1)
        right = jnp.concatenate([values[t] for t in rows], axis=0)
        return jnp.dot(left, right, preferred_element_type=jnp.float32)

    def add_block(index, hop):
        way, core = lax.div(index, 2), lax.rem(index, 2)
        block = place.origin_traced(way, hop) * 2 + core
        total = jnp.zeros_like(out_ref)
        if own_rows % TILE == 0:
            own_tiles = own_rows // TILE
            for k in range(0, own_tiles, 2):
                group = [block * own_tiles + j for j in range(k, min(k + 2, own_tiles))]
                total = total + product(group, own_all, group)
        for k in range(0, touched, 2):
            group = range(k, min(k + 2, touched))
            total = total + product(
                [tiles_smem[block, 0, j] for j in group],
                term_all,
                [block * touched + j for j in group],
            )
        out_ref[...] += total

    def absorb(hop):
        own.settle(hop)
        term.settle(hop)
        ways = 1 if hop in (0, place.hops) else 2

        def body(index, carry):
            add_block(index, hop)
            return carry

        lax.fori_loop(0, 2 * ways, body, 0)

    for hop in range(1, place.hops + 1):
        own.advance(hop)
        term.advance(hop)
        absorb(hop - 1)
    absorb(place.hops)
    if own_rows % TILE != 0:

        @pl.loop(0, columns_count)
        def add_own(t):
            rows = [t * per_tile + part for part in range(per_tile)]
            out_ref[...] += product([t], own_all, rows)

    for gather in (low, own, term, tiles):
        gather.finish()
    for crossing in crossings:
        crossing.wait_send()


def local(
    count,
    start_guess,
    right_side,
    root_diagonal,
    preconditioner,
    border_block,
    coupling_inverse,
    border_count,
    column_tiles,
):
    own_rows, half_rhs = start_guess.shape
    order = preconditioner.shape[1]
    half_rows, coupled = border_block.shape[1:]
    blocks = count * 2
    touched = column_tiles.shape[1]
    tiles_row = jnp.pad(column_tiles, ((0, 0), (0, 128 - touched)))[:, None, :]
    hops = count // 2
    ring_sems = []
    unit = math.gcd(own_rows, TILE)
    units = own_rows // unit
    for rows in (units, units, touched, 1):
        chunks = min(CHUNKS, rows)
        ring_sems += [pltpu.SemaphoreType.DMA((2 * (hops + 1) * chunks,))] * 4
    vmem = pl.BlockSpec(memory_space=pltpu.VMEM)
    smem = pl.BlockSpec(memory_space=pltpu.SMEM)
    anywhere = pl.BlockSpec(memory_space=pltpu.HBM)
    return pl.pallas_call(
        functools.partial(kernel, count),
        out_shape=jax.ShapeDtypeStruct((own_rows, half_rhs), jnp.float32),
        in_specs=[vmem, vmem, vmem, anywhere, anywhere, anywhere, smem, smem, vmem],
        out_specs=vmem,
        scratch_shapes=[
            pltpu.VMEM((order // unit, unit, half_rhs), jnp.bfloat16),
            pltpu.VMEM((order // unit, unit, half_rhs), jnp.bfloat16),
            pltpu.VMEM((blocks * touched, TILE, half_rhs), jnp.bfloat16),
            pltpu.VMEM((blocks, 1, 128), jnp.int32),
            pltpu.SMEM((blocks, 1, 128), jnp.int32),
            pltpu.VMEM((order // TILE, own_rows, TILE), jnp.bfloat16),
            pltpu.VMEM((2 * half_rows, coupled), jnp.bfloat16),
            pltpu.VMEM((2 * half_rows, 2 * half_rows), jnp.bfloat16),
            pltpu.SemaphoreType.DMA((4,)),
            pltpu.SemaphoreType.DMA((order // TILE,)),
            pltpu.SemaphoreType.DMA((2,)),
            pltpu.SemaphoreType.DMA((2,)),
        ]
        + ring_sems,
        compiler_params=pltpu.CompilerParams(
            collective_id=0, has_side_effects=True, vmem_limit_bytes=60 * 1024 * 1024
        ),
    )(
        start_guess,
        right_side,
        root_diagonal[None, :],
        preconditioner,
        border_block,
        coupling_inverse,
        border_count,
        column_tiles,
        tiles_row,
    )


def solution(mesh):
    rows = ("scen", "rootr")
    placed = (
        P(rows, "rootc"),
        P(rows, "rootc"),
        P(rows),
        P(rows, None),
        P(rows, "rootc", None),
        P(rows, "rootc", None),
        P(rows),
        P(rows, None),
    )
    return jax.shard_map(
        functools.partial(local, mesh.shape["scen"]),
        mesh=mesh,
        in_specs=placed,
        out_specs=P(rows, "rootc"),
        check_vma=False,
    )
```

profile of v0, /device:TPU:0, one launch (start us, length us, event | category | flops | bytes accessed | tf_op | source)
XLA Modules:
  0.0 59.0 jit_solution(8244544112330665478)
XLA Ops:
  0.7 1.2 %pad_bitcast_fusion.tiles_row_ref = s32[1,1,128]{2,1,0:T(1,128)} fusion(s32[1,6]{1,0:T(1,128)} %own_tiles_ref.1), kind=kLoop, calls=%fused_computation | loop fusion | bytes 536 | tf_op jit(solution)/shard_map/broadcast_in_dim | solution.py:323
  1.8 55.5 %shard_map.82 = f32[512,128]{1,0:T(8,128)} custom-call(f32[512,128]{1,0:T(8,128)} %guess_ref.1, f32[512,128]{1,0:T(8,128)} %right_ref.1, f32[1,512]{1,0:T(1,128)} %bitcast.3, bf16[512,8192]{1,0:T(8,128)(2,1)} %precon_hbm.1, bf16[1,256,768]{2,1,0:T(8,128)(2,1)} %border_hbm.1, bf16[1,256,512]{2,1,0:T(8,128)(2,1)} %inverse_hbm.1, s32[1]{0:T(128)S(6)} %copy.10.live_ref, ...), custom_call_target="tpu_custom_call" | custom-call | tf_op jit(solution)/shard_map/pallas_call | solution.py:334
  57.3 1.7 %copy.11 = f32[512,128]{1,0:T(8,128)} copy(f32[512,128]{1,0:T(8,128)} %shard_map.82) | data formatting | bytes 524288
where the time goes:
time: 59.2 us; the launch traced here: 59 us
  Pallas kernels  55.5 us (94%)
  local copies, waits for them, and re-layouts  2.84 us (5%)
  between operations  0.66 us (1%)
    pallas_call x1, Pallas kernels, local(): pl.pallas_call(functools.partial(kernel, count), out_shape=jax.ShapeDtype...  55.5 us
    unnamed x1, local copies, waits for them, and re-layouts  1.67 us

commit v1 on v0

v1 whole, which is shorter than its diff:
```python
import functools
import math

import jax
import jax.numpy as jnp
from jax import lax
from jax.experimental import pallas as pl
from jax.experimental.pallas import tpu as pltpu
from jax.sharding import PartitionSpec as P

TILE = 128
MESH = pl.DeviceIdType.MESH
LOW_STEP = 1
OWN_STEP = 1
TERM_STEP = 1
EARLY = 2


class Place:
    def __init__(self, count):
        self.count, self.hops = count, count // 2
        self.scen, self.core = lax.axis_index("scen"), lax.axis_index("rootr")
        side, level = lax.rem(self.scen, 2), lax.div(self.scen, 2)
        self.spot = level * (1 - side) + (count - 1 - level) * side
        self.ahead = [self.at(1), self.at(count - 1)]

    def at(self, shift):
        spot = lax.rem(self.spot + shift, self.count)
        upper = lax.div(spot, self.hops)
        return (1 - upper) * 2 * spot + upper * (2 * (self.count - 1 - spot) + 1)

    def origin(self, way, hop):
        return self.at(self.count - hop if way == 0 else hop)

    def origins(self, hop):
        if hop == 0:
            return [self.scen]
        if hop == self.hops:
            return [self.origin(0, hop)]
        return [self.origin(0, hop), self.origin(1, hop)]


class Stream:
    def __init__(self, place, buf, rows, step, sems):
        self.place, self.buf, self.rows, self.step = place, buf, rows, step
        self.chunks = rows // step
        self.ring_send, self.ring_recv, self.pair_send, self.pair_recv = sems
        self.ring_rows = self.pair_rows = 0

    def piece(self, scen, core, chunk):
        first = (scen * 2 + core) * self.rows + chunk * self.step
        return self.buf.at[pl.ds(first, self.step)]

    def carried(self, way, hop):
        if hop < self.place.hops:
            return range(self.chunks)
        half = (self.chunks + 1) // 2
        return range(half) if way == 0 else range(half, self.chunks)

    def rounds(self, hop, chunks=None):
        chunks = range(self.chunks) if chunks is None else chunks
        ways = [[(way, c) for c in self.carried(way, hop) if c in chunks] for way in range(2)]
        return [
            [way[i] for way in ways if i < len(way)] for i in range(max(len(way) for way in ways))
        ]

    def ring_copy(self, way, hop, chunk, scen):
        ref = self.piece(scen, self.place.core, chunk)
        return pltpu.make_async_remote_copy(
            src_ref=ref,
            dst_ref=ref,
            send_sem=self.ring_send.at[0],
            recv_sem=self.ring_recv.at[(way * self.place.hops + hop - 1) * self.chunks + chunk],
            device_id={"scen": self.place.ahead[way]},
            device_id_type=MESH,
        )

    def pair_copy(self, hop, ref):
        return pltpu.make_async_remote_copy(
            src_ref=ref,
            dst_ref=ref,
            send_sem=self.pair_send.at[0],
            recv_sem=self.pair_recv.at[hop],
            device_id={"rootr": 1 - self.place.core},
            device_id_type=MESH,
        )

    def send(self, way, hop, chunk, scen):
        if chunk in self.carried(way, hop):
            self.ring_copy(way, hop, chunk, scen).start()
            self.ring_rows += self.step

    def share(self, hop, chunk, scen):
        self.pair_copy(hop, self.piece(scen, self.place.core, chunk)).start()
        self.pair_rows += self.step

    def begin(self, chunks=None):
        for chunk in range(self.chunks) if chunks is None else chunks:
            for way in range(2):
                self.send(way, 1, chunk, self.place.scen)

    def begin_share(self):
        for chunk in range(self.chunks):
            self.share(0, chunk, self.place.scen)

    def arrive(self, hop, arrivals):
        for way, chunk in arrivals:
            scen = self.place.origin(way, hop)
            self.ring_copy(way, hop, chunk, scen).wait_recv()
            if hop < self.place.hops:
                self.send(way, hop + 1, chunk, scen)
            self.share(hop, chunk, scen)

    def settle(self, hop):
        whole = self.rows if hop in (0, self.place.hops) else 2 * self.rows
        self.pair_copy(hop, self.buf.at[pl.ds(0, whole)]).wait_recv()

    def finish(self):
        ref = self.buf.at[pl.ds(0, self.ring_rows)]
        pltpu.make_async_remote_copy(
            src_ref=ref,
            dst_ref=ref,
            send_sem=self.ring_send.at[0],
            recv_sem=self.ring_recv.at[0],
            device_id={"scen": self.place.ahead[0]},
            device_id_type=MESH,
        ).wait_send()
        self.pair_copy(0, self.buf.at[pl.ds(0, self.pair_rows)]).wait_send()


def kernel(
    count,
    guess_hbm,
    right_hbm,
    diagonal_hbm,
    precon_hbm,
    border_hbm,
    inverse_hbm,
    live_ref,
    own_tiles_ref,
    out_ref,
    guess,
    right,
    diagonal,
    low_all,
    own_all,
    term_all,
    tiles_all,
    tiles_smem,
    precon,
    border,
    inverse,
    local_sems,
    cross_send,
    cross_recv,
    *ring_sems,
):
    place = Place(count)
    hops = place.hops
    side = lax.axis_index("rootc")
    own_rows, half_rhs = guess.shape
    half_rows, coupled = border_hbm.shape[1:]
    touched = coupled // TILE
    own_block = place.scen * 2 + place.core

    barrier = pltpu.get_barrier_semaphore()
    peers = (
        {"scen": place.ahead[0]},
        {"scen": place.ahead[1]},
        {"rootr": 1 - place.core},
        {"rootc": 1 - side},
    )
    for peer in peers:
        pl.semaphore_signal(barrier, inc=1, device_id=peer, device_id_type=MESH)

    load_guess = pltpu.make_async_copy(guess_hbm, guess, local_sems.at[0])
    load_right = pltpu.make_async_copy(right_hbm, right, local_sems.at[1])
    load_diagonal = pltpu.make_async_copy(diagonal_hbm, diagonal, local_sems.at[2])
    own_half = pl.ds(pl.multiple_of(side * half_rows, half_rows), half_rows)
    load_border = pltpu.make_async_copy(border_hbm.at[0], border.at[own_half], local_sems.at[3])
    load_inverse = pltpu.make_async_copy(inverse_hbm.at[0], inverse.at[own_half], local_sems.at[4])
    columns_count = precon.shape[0]
    for load in (load_guess, load_right, load_diagonal, load_border, load_inverse):
        load.start()

    unit = low_all.shape[1]
    units = own_rows // unit
    per_tile = TILE // unit
    own_slice = pl.ds(own_block * units, units)
    split = (units, unit, half_rhs)
    lanes = lax.broadcasted_iota(jnp.int32, (1, 1, TILE), 2)
    tiles_row = jnp.zeros((1, 1, TILE), jnp.int32)
    for k in range(touched):
        tiles_row = jnp.where(lanes == k, own_tiles_ref[0, k], tiles_row)
    tiles_all[pl.ds(own_block, 1)] = tiles_row
    load_guess.wait()
    low_all[own_slice] = guess[...].astype(jnp.bfloat16).reshape(split)

    low = Stream(place, low_all, units, min(LOW_STEP, units), ring_sems[0:4])
    own = Stream(place, own_all, units, min(OWN_STEP, units), ring_sems[4:8])
    term = Stream(place, term_all, touched, TERM_STEP, ring_sems[8:12])
    tiles = Stream(place, tiles_all, 1, 1, ring_sems[12:16])
    early = range(min(EARLY, own.chunks))
    late = range(len(early), own.chunks)

    pl.semaphore_wait(barrier, len(peers))
    low.begin()
    crossings = []
    for index, (source, target) in enumerate(((border_hbm, border), (inverse_hbm, inverse))):
        crossing = pltpu.make_async_remote_copy(
            src_ref=source.at[0],
            dst_ref=target.at[own_half],
            send_sem=cross_send.at[index],
            recv_sem=cross_recv.at[index],
            device_id={"rootc": 1 - side},
            device_id_type=MESH,
        )
        crossing.start()
        crossings.append(crossing)
    low.begin_share()
    tiles.begin()

    load_right.wait()
    load_diagonal.wait()
    scale = jnp.broadcast_to(diagonal[...], (half_rhs, own_rows)).T
    own_terms = right[...] - scale * guess[...]
    own_all[own_slice] = own_terms.astype(jnp.bfloat16).reshape(split)
    own.begin(early)
    own.begin_share()
    tiles.begin_share()

    @pl.loop(0, columns_count)
    def start_column(t):
        columns = pl.ds(pl.multiple_of(t * TILE, TILE), TILE)
        pltpu.make_async_copy(precon_hbm.at[:, columns], precon.at[t], local_sems.at[5]).start()

    for hop in range(1, hops + 1):
        for arrivals in low.rounds(hop):
            low.arrive(hop, arrivals)
        for arrivals in tiles.rounds(hop):
            tiles.arrive(hop, arrivals)
        if hop == hops - 1:
            own.begin(late)
        if hop == hops:
            for arrivals in own.rounds(1, late):
                own.arrive(1, arrivals)
        for arrivals in own.rounds(hop, early):
            own.arrive(hop, arrivals)
    for hop in range(hops + 1):
        low.settle(hop)

    load_border.wait()
    crossings[0].wait_recv()
    live = jnp.clip(live_ref[0], 0, 2 * half_rows)
    live_mask = lax.broadcasted_iota(jnp.int32, (2 * half_rows, half_rhs), 0) < live
    picked = jnp.concatenate(
        [
            low_all[own_tiles_ref[0, k] * per_tile + part]
            for k in range(touched)
            for part in range(per_tile)
        ],
        axis=0,
    )
    values = jnp.dot(border[...], picked, preferred_element_type=jnp.float32)
    values = jnp.where(live_mask, values, 0.0).astype(jnp.bfloat16)
    load_inverse.wait()
    crossings[1].wait_recv()
    solved = jnp.dot(inverse[...], values, preferred_element_type=jnp.float32)
    solved = jnp.where(live_mask, solved, 0.0).astype(jnp.bfloat16)
    terms = lax.dot_general(
        border[...], solved, (((0,), (0,)), ((), ())), preferred_element_type=jnp.float32
    )
    term_all[pl.ds(own_block * touched, touched)] = terms.astype(jnp.bfloat16).reshape(
        touched, TILE, half_rhs
    )
    term.begin()
    term.begin_share()

    for hop in range(hops + 1):
        tiles.settle(hop)
    to_smem = pltpu.make_async_copy(tiles_all, tiles_smem, local_sems.at[6])
    to_smem.start()
    pltpu.make_async_copy(precon, precon, local_sems.at[5]).wait()
    out_ref[...] = guess[...]
    to_smem.wait()

    def product(columns, values, rows):
        left = jnp.concatenate([precon[t] for t in columns], axis=1)
        right = jnp.concatenate([values[t] for t in rows], axis=0)
        return jnp.dot(left, right, preferred_element_type=jnp.float32)

    own_tiles = own_rows // TILE

    def add_own(block):
        total = jnp.zeros_like(out_ref)
        for k in range(0, own_tiles, 2):
            group = [block * own_tiles + j for j in range(k, min(k + 2, own_tiles))]
            total = total + product(group, own_all, group)
        out_ref[...] += total

    def add_term(block):
        total = jnp.zeros_like(out_ref)
        for k in range(0, touched, 2):
            group = range(k, min(k + 2, touched))
            total = total + product(
                [tiles_smem[block, 0, j] for j in group],
                term_all,
                [block * touched + j for j in group],
            )
        out_ref[...] += total

    def work(stream, add, hop):
        blocks = [scen * 2 + core for core in range(2) for scen in place.origins(hop)]
        return [lambda: stream.settle(hop)] + [functools.partial(add, block) for block in blocks]

    def run(todo, count):
        for _ in range(min(count, len(todo))):
            todo.pop(0)()

    whole_tiles = own_rows % TILE == 0
    todo = work(own, add_own, 0) if whole_tiles else []
    for hop in range(1, hops + 1):
        todo += work(term, add_term, hop - 1)
        own_rounds = own.rounds(hop + 1, late) if hop < hops and late else []
        rounds = term.rounds(hop)
        if whole_tiles:
            todo += work(own, add_own, hop)
        share = -(-len(todo) // len(rounds))
        for arrivals in rounds:
            term.arrive(hop, arrivals)
            if own_rounds:
                own.arrive(hop + 1, own_rounds.pop(0))
            run(todo, share)
        for arrivals in own_rounds:
            own.arrive(hop + 1, arrivals)
        run(todo, len(todo))
    todo = work(term, add_term, hops)
    run(todo, len(todo))
    if not whole_tiles:
        for hop in range(hops + 1):
            own.settle(hop)

        @pl.loop(0, columns_count)
        def add_column(t):
            rows = [t * per_tile + part for part in range(per_tile)]
            out_ref[...] += product([t], own_all, rows)

    for stream in (low, own, term, tiles):
        stream.finish()
    for crossing in crossings:
        crossing.wait_send()


def local(
    count,
    start_guess,
    right_side,
    root_diagonal,
    preconditioner,
    border_block,
    coupling_inverse,
    border_count,
    column_tiles,
):
    own_rows, half_rhs = start_guess.shape
    order = preconditioner.shape[1]
    half_rows, coupled = border_block.shape[1:]
    blocks = count * 2
    touched = column_tiles.shape[1]
    hops = count // 2
    ring_sems = []
    unit = math.gcd(own_rows, TILE)
    units = own_rows // unit
    for rows, step in ((units, LOW_STEP), (units, OWN_STEP), (touched, TERM_STEP), (1, 1)):
        chunks = rows // min(step, rows)
        ring_sems += [
            pltpu.SemaphoreType.DMA((1,)),
            pltpu.SemaphoreType.DMA((2 * hops * chunks,)),
            pltpu.SemaphoreType.DMA((1,)),
            pltpu.SemaphoreType.DMA((hops + 1,)),
        ]
    vmem = pl.BlockSpec(memory_space=pltpu.VMEM)
    smem = pl.BlockSpec(memory_space=pltpu.SMEM)
    anywhere = pl.BlockSpec(memory_space=pltpu.HBM)
    return pl.pallas_call(
        functools.partial(kernel, count),
        out_shape=jax.ShapeDtypeStruct((own_rows, half_rhs), jnp.float32),
        in_specs=[anywhere] * 6 + [smem, smem],
        out_specs=vmem,
        scratch_shapes=[
            pltpu.VMEM((own_rows, half_rhs), jnp.float32),
            pltpu.VMEM((own_rows, half_rhs), jnp.float32),
            pltpu.VMEM((1, own_rows), jnp.float32),
            pltpu.VMEM((order // unit, unit, half_rhs), jnp.bfloat16),
            pltpu.VMEM((order // unit, unit, half_rhs), jnp.bfloat16),
            pltpu.VMEM((blocks * touched, TILE, half_rhs), jnp.bfloat16),
            pltpu.VMEM((blocks, 1, TILE), jnp.int32),
            pltpu.SMEM((blocks, 1, TILE), jnp.int32),
            pltpu.VMEM((order // TILE, own_rows, TILE), jnp.bfloat16),
            pltpu.VMEM((2 * half_rows, coupled), jnp.bfloat16),
            pltpu.VMEM((2 * half_rows, 2 * half_rows), jnp.bfloat16),
            pltpu.SemaphoreType.DMA((7,)),
            pltpu.SemaphoreType.DMA((2,)),
            pltpu.SemaphoreType.DMA((2,)),
        ]
        + ring_sems,
        compiler_params=pltpu.CompilerParams(
            collective_id=0, has_side_effects=True, vmem_limit_bytes=60 * 1024 * 1024
        ),
    )(
        start_guess,
        right_side,
        root_diagonal[None, :],
        preconditioner,
        border_block,
        coupling_inverse,
        border_count,
        column_tiles,
    )


def solution(mesh):
    rows = ("scen", "rootr")
    placed = (
        P(rows, "rootc"),
        P(rows, "rootc"),
        P(rows),
        P(rows, None),
        P(rows, "rootc", None),
        P(rows, "rootc", None),
        P(rows),
        P(rows, None),
    )
    return jax.shard_map(
        functools.partial(local, mesh.shape["scen"]),
        mesh=mesh,
        in_specs=placed,
        out_specs=P(rows, "rootc"),
        check_vma=False,
    )
```

time: 59.2 us -> 52.7 us (0.89)
  Pallas kernels: 55.5 us -> 50.1 us
  local copies, waits for them, and re-layouts: 2.84 us -> 1.67 us
    pallas_call x1, Pallas kernels: 55.5 us -> 50.1 us  [local(): pl.pallas_call(functools.partial(kernel, count), out_shape=jax.ShapeDtype...]
    broadcast_in_dim x1 -> x0, local copies, waits for them, and re-layouts: 1.17 us -> none  [local(): tiles_row = jnp.pad(column_tiles, ((0, 0), (0, 128 - touched)))[:, None, :]]
where the time goes in v1:
time: 52.7 us; the launch traced here: 52.4 us
  Pallas kernels  50.1 us (95%)
  local copies, waits for them, and re-layouts  1.67 us (3%)
  between operations  0.66 us (1%)
    pallas_call x1, Pallas kernels, local(): pl.pallas_call(functools.partial(kernel, count), out_shape=jax.ShapeDtype...  50.1 us
    unnamed x1, local copies, waits for them, and re-layouts  1.67 us

profile of v1, /device:TPU:0, one launch (start us, length us, event | category | flops | bytes accessed | tf_op | source)
XLA Modules:
  0.0 52.4 jit_solution(3924360498541599230)
XLA Ops:
  0.7 50.1 %shard_map.82 = f32[512,128]{1,0:T(8,128)} custom-call(f32[512,128]{1,0:T(8,128)} %guess_hbm.1, f32[512,128]{1,0:T(8,128)} %right_hbm.1, f32[1,512]{1,0:T(1,128)} %bitcast.1, bf16[512,8192]{1,0:T(8,128)(2,1)} %precon_hbm.1, bf16[1,256,768]{2,1,0:T(8,128)(2,1)} %border_hbm.1, bf16[1,256,512]{2,1,0:T(8,128)(2,1)} %inverse_hbm.1, s32[1]{0:T(128)S(6)} %copy.10.live_ref, ...), custom_call_target="tpu_custom_call" | custom-call | tf_op jit(solution)/shard_map/pallas_call | solution.py:385
  50.7 1.7 %copy.11 = f32[512,128]{1,0:T(8,128)} copy(f32[512,128]{1,0:T(8,128)} %shard_map.82) | data formatting | bytes 524288

commit v2 on v1

--- a/solution.py
+++ b/solution.py
@@ -11,9 +11,9 @@
 TILE = 128
 MESH = pl.DeviceIdType.MESH
 LOW_STEP = 1
-OWN_STEP = 1
-TERM_STEP = 1
-EARLY = 2
+OWN_STEP = 2
+TERM_STEP = 2
+AHEAD = 2
 
 
 class Place:
@@ -41,37 +41,39 @@
 
 
 class Stream:
-    def __init__(self, place, buf, rows, step, sems):
+    def __init__(self, place, hub, buf, rows, step, sems):
+        self.hub = hub
         self.place, self.buf, self.rows, self.step = place, buf, rows, step
         self.chunks = rows // step
         self.ring_send, self.ring_recv, self.pair_send, self.pair_recv = sems
-        self.ring_rows = self.pair_rows = 0
+        self.forwarded = self.shared = 0
 
     def piece(self, scen, core, chunk):
         first = (scen * 2 + core) * self.rows + chunk * self.step
         return self.buf.at[pl.ds(first, self.step)]
 
-    def carried(self, way, hop):
-        if hop < self.place.hops:
-            return range(self.chunks)
-        half = (self.chunks + 1) // 2
-        return range(half) if way == 0 else range(half, self.chunks)
-
-    def rounds(self, hop, chunks=None):
-        chunks = range(self.chunks) if chunks is None else chunks
-        ways = [[(way, c) for c in self.carried(way, hop) if c in chunks] for way in range(2)]
+    def carried(self, way, hop, core):
+        return hop < self.place.hops or way == core
+
+    def rounds(self, hop):
         return [
-            [way[i] for way in ways if i < len(way)] for i in range(max(len(way) for way in ways))
+            [
+                (way, core, chunk)
+                for core in (self.hub, 1 - self.hub)
+                for way in range(2)
+                if self.carried(way, hop, core)
+            ]
+            for chunk in range(self.chunks)
         ]
 
-    def ring_copy(self, way, hop, chunk, scen):
-        ref = self.piece(scen, self.place.core, chunk)
+    def ring_copy(self, way, hop, core, chunk, ref):
+        slot = ((way * self.place.hops + hop - 1) * 2 + core) * self.chunks + chunk
         return pltpu.make_async_remote_copy(
             src_ref=ref,
             dst_ref=ref,
             send_sem=self.ring_send.at[0],
-            recv_sem=self.ring_recv.at[(way * self.place.hops + hop - 1) * self.chunks + chunk],
-            device_id={"scen": self.place.ahead[way]},
+            recv_sem=self.ring_recv.at[slot],
+            device_id={"scen": self.place.ahead[way], "rootr": self.hub},
             device_id_type=MESH,
         )
 
@@ -85,47 +87,55 @@
             device_id_type=MESH,
         )
 
-    def send(self, way, hop, chunk, scen):
-        if chunk in self.carried(way, hop):
-            self.ring_copy(way, hop, chunk, scen).start()
-            self.ring_rows += self.step
-
-    def share(self, hop, chunk, scen):
-        self.pair_copy(hop, self.piece(scen, self.place.core, chunk)).start()
-        self.pair_rows += self.step
-
-    def begin(self, chunks=None):
-        for chunk in range(self.chunks) if chunks is None else chunks:
-            for way in range(2):
-                self.send(way, 1, chunk, self.place.scen)
-
-    def begin_share(self):
-        for chunk in range(self.chunks):
-            self.share(0, chunk, self.place.scen)
-
-    def arrive(self, hop, arrivals):
-        for way, chunk in arrivals:
-            scen = self.place.origin(way, hop)
-            self.ring_copy(way, hop, chunk, scen).wait_recv()
-            if hop < self.place.hops:
-                self.send(way, hop + 1, chunk, scen)
-            self.share(hop, chunk, scen)
+    def begin(self):
+        for core in range(2):
+
+            @pl.when(self.place.core == core)
+            def send():
+                for chunk in range(self.chunks):
+                    ref = self.piece(self.place.scen, core, chunk)
+                    for way in range(2):
+                        if self.carried(way, 1, core):
+                            self.ring_copy(way, 1, core, chunk, ref).start()
+
+        own = self.buf.at[pl.ds((self.place.scen * 2 + self.place.core) * self.rows, self.rows)]
+        self.pair_copy(0, own).start()
+
+    def relay(self, hop, arrivals):
+        for way, core, chunk in arrivals:
+            self.forwarded += self.step * (hop < self.place.hops and self.carried(way, hop + 1, core))
+            self.shared += self.step
+
+        @pl.when(self.place.core == self.hub)
+        def forward():
+            for way, core, chunk in arrivals:
+                ref = self.piece(self.place.origin(way, hop), core, chunk)
+                self.ring_copy(way, hop, core, chunk, ref).wait_recv()
+                if hop < self.place.hops and self.carried(way, hop + 1, core):
+                    self.ring_copy(way, hop + 1, core, chunk, ref).start()
+                self.pair_copy(hop, ref).start()
 
     def settle(self, hop):
-        whole = self.rows if hop in (0, self.place.hops) else 2 * self.rows
-        self.pair_copy(hop, self.buf.at[pl.ds(0, whole)]).wait_recv()
+        if hop == 0:
+            self.pair_copy(0, self.buf.at[pl.ds(0, self.rows)]).wait_recv()
+            return
+
+        @pl.when(self.place.core != self.hub)
+        def arrived():
+            rows = (2 if hop == self.place.hops else 4) * self.rows
+            self.pair_copy(hop, self.buf.at[pl.ds(0, rows)]).wait_recv()
 
     def finish(self):
-        ref = self.buf.at[pl.ds(0, self.ring_rows)]
-        pltpu.make_async_remote_copy(
-            src_ref=ref,
-            dst_ref=ref,
-            send_sem=self.ring_send.at[0],
-            recv_sem=self.ring_recv.at[0],
-            device_id={"scen": self.place.ahead[0]},
-            device_id_type=MESH,
-        ).wait_send()
-        self.pair_copy(0, self.buf.at[pl.ds(0, self.pair_rows)]).wait_send()
+        for core in range(2):
+            ways = sum(self.carried(way, 1, core) for way in range(2))
+            ring_rows = ways * self.rows + (core == self.hub) * self.forwarded
+            pair_rows = self.rows + (core == self.hub) * self.shared
+
+            @pl.when(self.place.core == core)
+            def sent():
+                ref = self.buf.at[pl.ds(0, ring_rows)]
+                self.ring_copy(0, 1, 0, 0, ref).wait_send()
+                self.pair_copy(0, self.buf.at[pl.ds(0, pair_rows)]).wait_send()
 
 
 def kernel(
@@ -164,12 +174,8 @@
     own_block = place.scen * 2 + place.core
 
     barrier = pltpu.get_barrier_semaphore()
-    peers = (
-        {"scen": place.ahead[0]},
-        {"scen": place.ahead[1]},
-        {"rootr": 1 - place.core},
-        {"rootc": 1 - side},
-    )
+    peers = [{"scen": scen, "rootr": core} for scen in place.ahead for core in range(2)]
+    peers += [{"rootr": 1 - place.core}, {"rootc": 1 - side}]
     for peer in peers:
         pl.semaphore_signal(barrier, inc=1, device_id=peer, device_id_type=MESH)
 
@@ -196,12 +202,10 @@
     load_guess.wait()
     low_all[own_slice] = guess[...].astype(jnp.bfloat16).reshape(split)
 
-    low = Stream(place, low_all, units, min(LOW_STEP, units), ring_sems[0:4])
-    own = Stream(place, own_all, units, min(OWN_STEP, units), ring_sems[4:8])
-    term = Stream(place, term_all, touched, TERM_STEP, ring_sems[8:12])
-    tiles = Stream(place, tiles_all, 1, 1, ring_sems[12:16])
-    early = range(min(EARLY, own.chunks))
-    late = range(len(early), own.chunks)
+    low = Stream(place, 1, low_all, units, min(LOW_STEP, units), ring_sems[0:4])
+    own = Stream(place, 0, own_all, units, min(OWN_STEP, units), ring_sems[4:8])
+    term = Stream(place, 1, term_all, touched, TERM_STEP, ring_sems[8:12])
+    tiles = Stream(place, 1, tiles_all, 1, 1, ring_sems[12:16])
 
     pl.semaphore_wait(barrier, len(peers))
     low.begin()
@@ -217,7 +221,6 @@
         )
         crossing.start()
         crossings.append(crossing)
-    low.begin_share()
     tiles.begin()
 
     load_right.wait()
@@ -225,9 +228,6 @@
     scale = jnp.broadcast_to(diagonal[...], (half_rhs, own_rows)).T
     own_terms = right[...] - scale * guess[...]
     own_all[own_slice] = own_terms.astype(jnp.bfloat16).reshape(split)
-    own.begin(early)
-    own.begin_share()
-    tiles.begin_share()
 
     @pl.loop(0, columns_count)
     def start_column(t):
@@ -236,18 +236,22 @@
 
     for hop in range(1, hops + 1):
         for arrivals in low.rounds(hop):
-            low.arrive(hop, arrivals)
+            low.relay(hop, arrivals)
+        if hop == max(hops - AHEAD, 1):
+            low.settle(hop)
+            own.begin()
         for arrivals in tiles.rounds(hop):
-            tiles.arrive(hop, arrivals)
-        if hop == hops - 1:
-            own.begin(late)
-        if hop == hops:
-            for arrivals in own.rounds(1, late):
-                own.arrive(1, arrivals)
-        for arrivals in own.rounds(hop, early):
-            own.arrive(hop, arrivals)
+            tiles.relay(hop, arrivals)
+    flow = [(hop, arrivals) for hop in range(1, hops + 1) for arrivals in own.rounds(hop)]
+
+    def drain(stop):
+        while flow and flow[0][0] <= stop:
+            own.relay(*flow.pop(0))
+
+    drain(1)
     for hop in range(hops + 1):
-        low.settle(hop)
+        if hop != max(hops - AHEAD, 1):
+            low.settle(hop)
 
     load_border.wait()
     crossings[0].wait_recv()
@@ -263,6 +267,7 @@
     )
     values = jnp.dot(border[...], picked, preferred_element_type=jnp.float32)
     values = jnp.where(live_mask, values, 0.0).astype(jnp.bfloat16)
+    drain(2)
     load_inverse.wait()
     crossings[1].wait_recv()
     solved = jnp.dot(inverse[...], values, preferred_element_type=jnp.float32)
@@ -274,7 +279,6 @@
         touched, TILE, half_rhs
     )
     term.begin()
-    term.begin_share()
 
     for hop in range(hops + 1):
         tiles.settle(hop)
@@ -321,18 +325,18 @@
     todo = work(own, add_own, 0) if whole_tiles else []
     for hop in range(1, hops + 1):
         todo += work(term, add_term, hop - 1)
-        own_rounds = own.rounds(hop + 1, late) if hop < hops and late else []
-        rounds = term.rounds(hop)
         if whole_tiles:
             todo += work(own, add_own, hop)
+        rounds = term.rounds(hop)
         share = -(-len(todo) // len(rounds))
         for arrivals in rounds:
-            term.arrive(hop, arrivals)
-            if own_rounds:
-                own.arrive(hop + 1, own_rounds.pop(0))
+            if flow:
+                own.relay(*flow.pop(0))
+            term.relay(hop, arrivals)
+            if flow and flow[0][0] <= hop:
+                own.relay(*flow.pop(0))
             run(todo, share)
-        for arrivals in own_rounds:
-            own.arrive(hop + 1, arrivals)
+        drain(hop + 1)
         run(todo, len(todo))
     todo = work(term, add_term, hops)
     run(todo, len(todo))
@@ -345,6 +349,7 @@
             rows = [t * per_tile + part for part in range(per_tile)]
             out_ref[...] += product([t], own_all, rows)
 
+    drain(hops)
     for stream in (low, own, term, tiles):
         stream.finish()
     for crossing in crossings:
@@ -375,7 +380,7 @@
         chunks = rows // min(step, rows)
         ring_sems += [
             pltpu.SemaphoreType.DMA((1,)),
-            pltpu.SemaphoreType.DMA((2 * hops * chunks,)),
+            pltpu.SemaphoreType.DMA((4 * hops * chunks,)),
             pltpu.SemaphoreType.DMA((1,)),
             pltpu.SemaphoreType.DMA((hops + 1,)),
         ]
@@ -384,7 +389,7 @@
     anywhere = pl.BlockSpec(memory_space=pltpu.HBM)
     return pl.pallas_call(
         functools.partial(kernel, count),
-        out_shape=jax.ShapeDtypeStruct((own_rows, half_rhs), jnp.float32),
+        out_shape=pltpu.VMEM((own_rows, half_rhs), jnp.float32),
         in_specs=[anywhere] * 6 + [smem, smem],
         out_specs=vmem,
         scratch_shapes=[

time: 52.7 us -> 48.4 us (0.918)
  Pallas kernels: 50.1 us -> 46.8 us
  local copies, waits for them, and re-layouts: 1.67 us -> 0.71 us
    pallas_call x1, Pallas kernels: 50.1 us -> 46.8 us  [local(): pl.pallas_call(functools.partial(kernel, count), out_shape=pltpu.VMEM((ow...]
    unnamed x1, local copies, waits for them, and re-layouts: 1.67 us -> 0.71 us
where the time goes in v2:
time: 48.4 us; the launch traced here: 48.2 us
  Pallas kernels  46.8 us (97%)
  local copies, waits for them, and re-layouts  0.71 us (1%)
  between operations  0.66 us (1%)
    pallas_call x1, Pallas kernels, local(): pl.pallas_call(functools.partial(kernel, count), out_shape=pltpu.VMEM((ow...  46.8 us

profile of v2, /device:TPU:0, one launch (start us, length us, event | category | flops | bytes accessed | tf_op | source)
XLA Modules:
  0.0 48.2 jit_solution(6981621946864186389)
XLA Ops:
  0.7 46.8 %shard_map.82 = f32[512,128]{1,0:T(8,128)S(1)} custom-call(f32[512,128]{1,0:T(8,128)} %guess_hbm.1, f32[512,128]{1,0:T(8,128)} %right_hbm.1, f32[1,512]{1,0:T(1,128)} %bitcast.1, bf16[512,8192]{1,0:T(8,128)(2,1)} %precon_hbm.1, bf16[1,256,768]{2,1,0:T(8,128)(2,1)} %border_hbm.1, bf16[1,256,512]{2,1,0:T(8,128)(2,1)} %inverse_hbm.1, s32[1]{0:T(128)S(6)} %copy.11.live_ref, ...), custom_call_target="tpu_custom_call" | custom-call | tf_op jit(solution)/shard_map/pallas_call | solution.py:390
  47.5 0.7 %copy.10 = f32[512,128]{1,0:T(8,128)} copy(f32[512,128]{1,0:T(8,128)S(1)} %shard_map.82) | data formatting | bytes 524288

commit v3 on v2

--- a/solution.py
+++ b/solution.py
@@ -1,4 +1,5 @@
 import functools
+import itertools
 import math
 
 import jax
@@ -87,19 +88,24 @@
             device_id_type=MESH,
         )
 
-    def begin(self):
+    def send(self, chunks):
         for core in range(2):
 
             @pl.when(self.place.core == core)
-            def send():
-                for chunk in range(self.chunks):
+            def start():
+                for chunk in chunks:
                     ref = self.piece(self.place.scen, core, chunk)
                     for way in range(2):
                         if self.carried(way, 1, core):
                             self.ring_copy(way, 1, core, chunk, ref).start()
 
+    def share(self):
         own = self.buf.at[pl.ds((self.place.scen * 2 + self.place.core) * self.rows, self.rows)]
         self.pair_copy(0, own).start()
+
+    def begin(self):
+        self.send(range(self.chunks))
+        self.share()
 
     def relay(self, hop, arrivals):
         for way, core, chunk in arrivals:
@@ -113,17 +119,24 @@
                 self.ring_copy(way, hop, core, chunk, ref).wait_recv()
                 if hop < self.place.hops and self.carried(way, hop + 1, core):
                     self.ring_copy(way, hop + 1, core, chunk, ref).start()
-                self.pair_copy(hop, ref).start()
-
-    def settle(self, hop):
+                self.pair_copy(self.pair_slot(hop, chunk), ref).start()
+
+    def pair_slot(self, hop, chunk):
+        return hop + chunk * (hop == self.place.hops)
+
+    def settle(self, hop, chunks=None):
         if hop == 0:
             self.pair_copy(0, self.buf.at[pl.ds(0, self.rows)]).wait_recv()
             return
 
         @pl.when(self.place.core != self.hub)
         def arrived():
-            rows = (2 if hop == self.place.hops else 4) * self.rows
-            self.pair_copy(hop, self.buf.at[pl.ds(0, rows)]).wait_recv()
+            if hop < self.place.hops:
+                self.pair_copy(hop, self.buf.at[pl.ds(0, 4 * self.rows)]).wait_recv()
+                return
+            for chunk in range(self.chunks) if chunks is None else chunks:
+                ref = self.buf.at[pl.ds(0, 2 * self.step)]
+                self.pair_copy(self.pair_slot(hop, chunk), ref).wait_recv()
 
     def finish(self):
         for core in range(2):
@@ -146,9 +159,11 @@
     precon_hbm,
     border_hbm,
     inverse_hbm,
+    live_hbm,
+    own_tiles_hbm,
+    out_ref,
     live_ref,
     own_tiles_ref,
-    out_ref,
     guess,
     right,
     diagonal,
@@ -185,8 +200,11 @@
     own_half = pl.ds(pl.multiple_of(side * half_rows, half_rows), half_rows)
     load_border = pltpu.make_async_copy(border_hbm.at[0], border.at[own_half], local_sems.at[3])
     load_inverse = pltpu.make_async_copy(inverse_hbm.at[0], inverse.at[own_half], local_sems.at[4])
+    load_live = pltpu.make_async_copy(live_hbm, live_ref, local_sems.at[7])
+    load_tiles = pltpu.make_async_copy(own_tiles_hbm, own_tiles_ref, local_sems.at[8])
     columns_count = precon.shape[0]
-    for load in (load_guess, load_right, load_diagonal, load_border, load_inverse):
+    loads = (load_guess, load_tiles, load_right, load_diagonal, load_border, load_inverse, load_live)
+    for load in loads:
         load.start()
 
     unit = low_all.shape[1]
@@ -194,11 +212,6 @@
     per_tile = TILE // unit
     own_slice = pl.ds(own_block * units, units)
     split = (units, unit, half_rhs)
-    lanes = lax.broadcasted_iota(jnp.int32, (1, 1, TILE), 2)
-    tiles_row = jnp.zeros((1, 1, TILE), jnp.int32)
-    for k in range(touched):
-        tiles_row = jnp.where(lanes == k, own_tiles_ref[0, k], tiles_row)
-    tiles_all[pl.ds(own_block, 1)] = tiles_row
     load_guess.wait()
     low_all[own_slice] = guess[...].astype(jnp.bfloat16).reshape(split)
 
@@ -221,6 +234,12 @@
         )
         crossing.start()
         crossings.append(crossing)
+    load_tiles.wait()
+    lanes = lax.broadcasted_iota(jnp.int32, (1, 1, TILE), 2)
+    tiles_row = jnp.zeros((1, 1, TILE), jnp.int32)
+    for k in range(touched):
+        tiles_row = jnp.where(lanes == k, own_tiles_ref[0, k], tiles_row)
+    tiles_all[pl.ds(own_block, 1)] = tiles_row
     tiles.begin()
 
     load_right.wait()
@@ -250,11 +269,54 @@
 
     drain(1)
     for hop in range(hops + 1):
+        if hop == hops:
+            own.relay(*flow.pop(0))
         if hop != max(hops - AHEAD, 1):
             low.settle(hop)
 
+    def product(columns, values, rows):
+        left = jnp.concatenate([precon[t] for t in columns], axis=1)
+        right = jnp.concatenate([values[t] for t in rows], axis=0)
+        return jnp.dot(left, right, preferred_element_type=jnp.float32)
+
+    own_tiles = own_rows // TILE
+
+    def add_own(block):
+        total = jnp.zeros_like(out_ref)
+        for k in range(0, own_tiles, 2):
+            group = [block * own_tiles + j for j in range(k, min(k + 2, own_tiles))]
+            total = total + product(group, own_all, group)
+        out_ref[...] += total
+
+    def add_term(*blocks, tiles=range(touched)):
+        total = jnp.zeros_like(out_ref)
+        for block, k in itertools.product(blocks, tiles[::2]):
+            group = range(k, min(k + 2, tiles[-1] + 1))
+            total = total + product(
+                [tiles_smem[block, 0, j] for j in group],
+                term_all,
+                [block * touched + j for j in group],
+            )
+        out_ref[...] += total
+
+    def work(stream, add, hop):
+        blocks = [scen * 2 + core for core in range(2) for scen in place.origins(hop)]
+        return [lambda: stream.settle(hop)] + [functools.partial(add, block) for block in blocks]
+
+    def add_last(chunk):
+        term.settle(hops, [chunk])
+        last = place.origin(0, hops) * 2
+        tiles = range(chunk * term.step, (chunk + 1) * term.step)
+        add_term(last, last + 1, tiles=tiles)
+
+    def run(todo, count):
+        for _ in range(min(count, len(todo))):
+            todo.pop(0)()
+
+    whole_tiles = own_rows % TILE == 0
     load_border.wait()
     crossings[0].wait_recv()
+    load_live.wait()
     live = jnp.clip(live_ref[0], 0, 2 * half_rows)
     live_mask = lax.broadcasted_iota(jnp.int32, (2 * half_rows, half_rhs), 0) < live
     picked = jnp.concatenate(
@@ -268,64 +330,38 @@
     values = jnp.dot(border[...], picked, preferred_element_type=jnp.float32)
     values = jnp.where(live_mask, values, 0.0).astype(jnp.bfloat16)
     drain(2)
+    pltpu.make_async_copy(precon, precon, local_sems.at[5]).wait()
+    out_ref[...] = guess[...]
+    todo = work(own, add_own, 0) + work(own, add_own, 1) if whole_tiles else []
+    run(todo, len(todo))
     load_inverse.wait()
     crossings[1].wait_recv()
     solved = jnp.dot(inverse[...], values, preferred_element_type=jnp.float32)
     solved = jnp.where(live_mask, solved, 0.0).astype(jnp.bfloat16)
-    terms = lax.dot_general(
-        border[...], solved, (((0,), (0,)), ((), ())), preferred_element_type=jnp.float32
-    )
-    term_all[pl.ds(own_block * touched, touched)] = terms.astype(jnp.bfloat16).reshape(
-        touched, TILE, half_rhs
-    )
-    term.begin()
+    width = term.step * TILE
+    for chunk in range(term.chunks):
+        left = border[:, pl.ds(chunk * width, width)]
+        terms = lax.dot_general(
+            left, solved, (((0,), (0,)), ((), ())), preferred_element_type=jnp.float32
+        )
+        term_all[pl.ds(own_block * touched + chunk * term.step, term.step)] = terms.astype(
+            jnp.bfloat16
+        ).reshape(term.step, TILE, half_rhs)
+        if chunk:
+            term.send([chunk - 1])
+    term.send([term.chunks - 1])
+    term.share()
 
     for hop in range(hops + 1):
         tiles.settle(hop)
     to_smem = pltpu.make_async_copy(tiles_all, tiles_smem, local_sems.at[6])
     to_smem.start()
-    pltpu.make_async_copy(precon, precon, local_sems.at[5]).wait()
-    out_ref[...] = guess[...]
     to_smem.wait()
 
-    def product(columns, values, rows):
-        left = jnp.concatenate([precon[t] for t in columns], axis=1)
-        right = jnp.concatenate([values[t] for t in rows], axis=0)
-        return jnp.dot(left, right, preferred_element_type=jnp.float32)
-
-    own_tiles = own_rows // TILE
-
-    def add_own(block):
-        total = jnp.zeros_like(out_ref)
-        for k in range(0, own_tiles, 2):
-            group = [block * own_tiles + j for j in range(k, min(k + 2, own_tiles))]
-            total = total + product(group, own_all, group)
-        out_ref[...] += total
-
-    def add_term(block):
-        total = jnp.zeros_like(out_ref)
-        for k in range(0, touched, 2):
-            group = range(k, min(k + 2, touched))
-            total = total + product(
-                [tiles_smem[block, 0, j] for j in group],
-                term_all,
-                [block * touched + j for j in group],
-            )
-        out_ref[...] += total
-
-    def work(stream, add, hop):
-        blocks = [scen * 2 + core for core in range(2) for scen in place.origins(hop)]
-        return [lambda: stream.settle(hop)] + [functools.partial(add, block) for block in blocks]
-
-    def run(todo, count):
-        for _ in range(min(count, len(todo))):
-            todo.pop(0)()
-
-    whole_tiles = own_rows % TILE == 0
-    todo = work(own, add_own, 0) if whole_tiles else []
+    todo = []
     for hop in range(1, hops + 1):
         todo += work(term, add_term, hop - 1)
-        if whole_tiles:
+        if whole_tiles and hop > 1:
             todo += work(own, add_own, hop)
         rounds = term.rounds(hop)
         share = -(-len(todo) // len(rounds))
@@ -336,10 +372,11 @@
             if flow and flow[0][0] <= hop:
                 own.relay(*flow.pop(0))
             run(todo, share)
+            if hop == hops and arrivals[0][2]:
+                add_last(arrivals[0][2] - 1)
         drain(hop + 1)
         run(todo, len(todo))
-    todo = work(term, add_term, hops)
-    run(todo, len(todo))
+    add_last(term.chunks - 1)
     if not whole_tiles:
         for hop in range(hops + 1):
             own.settle(hop)
@@ -382,17 +419,18 @@
             pltpu.SemaphoreType.DMA((1,)),
             pltpu.SemaphoreType.DMA((4 * hops * chunks,)),
             pltpu.SemaphoreType.DMA((1,)),
-            pltpu.SemaphoreType.DMA((hops + 1,)),
+            pltpu.SemaphoreType.DMA((hops + chunks,)),
         ]
     vmem = pl.BlockSpec(memory_space=pltpu.VMEM)
-    smem = pl.BlockSpec(memory_space=pltpu.SMEM)
     anywhere = pl.BlockSpec(memory_space=pltpu.HBM)
     return pl.pallas_call(
         functools.partial(kernel, count),
         out_shape=pltpu.VMEM((own_rows, half_rhs), jnp.float32),
-        in_specs=[anywhere] * 6 + [smem, smem],
+        in_specs=[anywhere] * 8,
         out_specs=vmem,
         scratch_shapes=[
+            pltpu.SMEM(border_count.shape, jnp.int32),
+            pltpu.SMEM(column_tiles.shape, jnp.int32),
             pltpu.VMEM((own_rows, half_rhs), jnp.float32),
             pltpu.VMEM((own_rows, half_rhs), jnp.float32),
             pltpu.VMEM((1, own_rows), jnp.float32),
@@ -404,7 +442,7 @@
             pltpu.VMEM((order // TILE, own_rows, TILE), jnp.bfloat16),
             pltpu.VMEM((2 * half_rows, coupled), jnp.bfloat16),
             pltpu.VMEM((2 * half_rows, 2 * half_rows), jnp.bfloat16),
-            pltpu.SemaphoreType.DMA((7,)),
+            pltpu.SemaphoreType.DMA((9,)),
             pltpu.SemaphoreType.DMA((2,)),
             pltpu.SemaphoreType.DMA((2,)),
         ]

time: 48.4 us -> 47.3 us (0.977)
  Pallas kernels: 46.8 us -> 45.8 us
    pallas_call x1, Pallas kernels: 46.8 us -> 45.8 us  [local(): pl.pallas_call(functools.partial(kernel, count), out_shape=pltpu.VMEM((ow...]
where the time goes in v3:
time: 47.3 us; the launch traced here: 47.1 us
  Pallas kernels  45.8 us (97%)
  local copies, waits for them, and re-layouts  0.71 us (2%)
  between operations  0.66 us (1%)
    pallas_call x1, Pallas kernels, local(): pl.pallas_call(functools.partial(kernel, count), out_shape=pltpu.VMEM((ow...  45.8 us

profile of v3, /device:TPU:0, one launch (start us, length us, event | category | flops | bytes accessed | tf_op | source)
XLA Modules:
  0.0 47.1 jit_solution(2993208879938314459)
XLA Ops:
  0.7 45.8 %shard_map.82 = f32[512,128]{1,0:T(8,128)S(1)} custom-call(f32[512,128]{1,0:T(8,128)} %guess_hbm.1, f32[512,128]{1,0:T(8,128)} %right_hbm.1, f32[1,512]{1,0:T(1,128)} %bitcast.1, bf16[512,8192]{1,0:T(8,128)(2,1)} %precon_hbm.1, bf16[1,256,768]{2,1,0:T(8,128)(2,1)} %border_hbm.1, bf16[1,256,512]{2,1,0:T(8,128)(2,1)} %inverse_hbm.1, s32[1]{0:T(128)S(6)} %copy.11.live_hbm, ...), custom_call_target="tpu_custom_call" | custom-call | tf_op jit(solution)/shard_map/pallas_call | solution.py:426
  46.4 0.7 %copy.10 = f32[512,128]{1,0:T(8,128)} copy(f32[512,128]{1,0:T(8,128)S(1)} %shard_map.82) | data formatting | bytes 524288

commit v4 on v3

--- a/solution.py
+++ b/solution.py
@@ -317,7 +317,7 @@
     load_border.wait()
     crossings[0].wait_recv()
     load_live.wait()
-    live = jnp.clip(live_ref[0], 0, 2 * half_rows)
+    live = jnp.clip(live_ref[0, 0], 0, 2 * half_rows)
     live_mask = lax.broadcasted_iota(jnp.int32, (2 * half_rows, half_rhs), 0) < live
     picked = jnp.concatenate(
         [
@@ -361,8 +361,8 @@
     todo = []
     for hop in range(1, hops + 1):
         todo += work(term, add_term, hop - 1)
-        if whole_tiles and hop > 1:
-            todo += work(own, add_own, hop)
+        if whole_tiles and hop < hops:
+            todo = work(own, add_own, hop + 1) + todo
         rounds = term.rounds(hop)
         share = -(-len(todo) // len(rounds))
         for arrivals in rounds:
@@ -429,7 +429,7 @@
         in_specs=[anywhere] * 8,
         out_specs=vmem,
         scratch_shapes=[
-            pltpu.SMEM(border_count.shape, jnp.int32),
+            pltpu.SMEM((1,) + border_count.shape, jnp.int32),
             pltpu.SMEM(column_tiles.shape, jnp.int32),
             pltpu.VMEM((own_rows, half_rhs), jnp.float32),
             pltpu.VMEM((own_rows, half_rhs), jnp.float32),
@@ -457,7 +457,7 @@
         preconditioner,
         border_block,
         coupling_inverse,
-        border_count,
+        border_count[None, :],
         column_tiles,
     )
 

time: 47.3 us -> 47 us (level)
  no operation moved by 1% of the time
where the time goes in v4:
time: 47 us; the launch traced here: 46.9 us
  Pallas kernels  45.5 us (97%)
  local copies, waits for them, and re-layouts  0.71 us (2%)
  between operations  0.66 us (1%)
    pallas_call x1, Pallas kernels, local(): pl.pallas_call(functools.partial(kernel, count), out_shape=pltpu.VMEM((ow...  45.5 us

profile of v4, /device:TPU:0, one launch (start us, length us, event | category | flops | bytes accessed | tf_op | source)
XLA Modules:
  0.0 46.9 jit_solution(10543757395105310402)
XLA Ops:
  0.7 45.5 %shard_map.82 = f32[512,128]{1,0:T(8,128)S(1)} custom-call(f32[512,128]{1,0:T(8,128)} %guess_hbm.1, f32[512,128]{1,0:T(8,128)} %right_hbm.1, f32[1,512]{1,0:T(1,128)} %bitcast.3, bf16[512,8192]{1,0:T(8,128)(2,1)} %precon_hbm.1, bf16[1,256,768]{2,1,0:T(8,128)(2,1)} %border_hbm.1, bf16[1,256,512]{2,1,0:T(8,128)(2,1)} %inverse_hbm.1, s32[1,1]{1,0:T(1,128)} %bitcast.2.live_hbm, ...), custom_call_target="tpu_custom_call" | custom-call | tf_op jit(solution)/shard_map/pallas_call | solution.py:426
  46.2 0.7 %copy.10 = f32[512,128]{1,0:T(8,128)} copy(f32[512,128]{1,0:T(8,128)S(1)} %shard_map.82) | data formatting | bytes 524288

commit v5 on v4

--- a/solution.py
+++ b/solution.py
@@ -175,6 +175,7 @@
     precon,
     border,
     inverse,
+    near_terms,
     local_sems,
     cross_send,
     cross_recv,
@@ -329,21 +330,34 @@
     )
     values = jnp.dot(border[...], picked, preferred_element_type=jnp.float32)
     values = jnp.where(live_mask, values, 0.0).astype(jnp.bfloat16)
+    load_inverse.wait()
+
+    def solve(start):
+        rows = pl.ds(pl.multiple_of(start, half_rows), half_rows)
+        rows_live = lax.broadcasted_iota(jnp.int32, (half_rows, half_rhs), 0) + start < live
+        part = jnp.dot(inverse[rows], values, preferred_element_type=jnp.float32)
+        return rows, jnp.where(rows_live, part, 0.0).astype(jnp.bfloat16)
+
+    def couple(rows, part, columns):
+        return lax.dot_general(
+            border[rows, columns],
+            part,
+            (((0,), (0,)), ((), ())),
+            preferred_element_type=jnp.float32,
+        )
+
     drain(2)
+    near_terms[...] = couple(*solve(side * half_rows), pl.ds(0, coupled))
     pltpu.make_async_copy(precon, precon, local_sems.at[5]).wait()
     out_ref[...] = guess[...]
     todo = work(own, add_own, 0) + work(own, add_own, 1) if whole_tiles else []
     run(todo, len(todo))
-    load_inverse.wait()
     crossings[1].wait_recv()
-    solved = jnp.dot(inverse[...], values, preferred_element_type=jnp.float32)
-    solved = jnp.where(live_mask, solved, 0.0).astype(jnp.bfloat16)
+    far = solve((1 - side) * half_rows)
     width = term.step * TILE
     for chunk in range(term.chunks):
-        left = border[:, pl.ds(chunk * width, width)]
-        terms = lax.dot_general(
-            left, solved, (((0,), (0,)), ((), ())), preferred_element_type=jnp.float32
-        )
+        columns = pl.ds(chunk * width, width)
+        terms = near_terms[columns] + couple(*far, columns)
         term_all[pl.ds(own_block * touched + chunk * term.step, term.step)] = terms.astype(
             jnp.bfloat16
         ).reshape(term.step, TILE, half_rhs)
@@ -442,6 +456,7 @@
             pltpu.VMEM((order // TILE, own_rows, TILE), jnp.bfloat16),
             pltpu.VMEM((2 * half_rows, coupled), jnp.bfloat16),
             pltpu.VMEM((2 * half_rows, 2 * half_rows), jnp.bfloat16),
+            pltpu.VMEM((coupled, half_rhs), jnp.float32),
             pltpu.SemaphoreType.DMA((9,)),
             pltpu.SemaphoreType.DMA((2,)),
             pltpu.SemaphoreType.DMA((2,)),

time: 47 us -> 46.9 us (level)
  no operation moved by 1% of the time
where the time goes in v5:
time: 46.9 us; the launch traced here: 46.8 us
  Pallas kernels  45.4 us (97%)
  local copies, waits for them, and re-layouts  0.71 us (2%)
  between operations  0.66 us (1%)
    pallas_call x1, Pallas kernels, local(): pl.pallas_call(functools.partial(kernel, count), out_shape=pltpu.VMEM((ow...  45.4 us

profile of v5, /device:TPU:0, one launch (start us, length us, event | category | flops | bytes accessed | tf_op | source)
XLA Modules:
  0.0 46.8 jit_solution(5025895154376142942)
XLA Ops:
  0.7 45.4 %shard_map.82 = f32[512,128]{1,0:T(8,128)S(1)} custom-call(f32[512,128]{1,0:T(8,128)} %guess_hbm.1, f32[512,128]{1,0:T(8,128)} %right_hbm.1, f32[1,512]{1,0:T(1,128)} %bitcast.3, bf16[512,8192]{1,0:T(8,128)(2,1)} %precon_hbm.1, bf16[1,256,768]{2,1,0:T(8,128)(2,1)} %border_hbm.1, bf16[1,256,512]{2,1,0:T(8,128)(2,1)} %inverse_hbm.1, s32[1,1]{1,0:T(1,128)} %bitcast.2.live_hbm, ...), custom_call_target="tpu_custom_call" | custom-call | tf_op jit(solution)/shard_map/pallas_call | solution.py:440
  46.1 0.7 %copy.10 = f32[512,128]{1,0:T(8,128)} copy(f32[512,128]{1,0:T(8,128)S(1)} %shard_map.82) | data formatting | bytes 524288

commit v6 on v5

--- a/solution.py
+++ b/solution.py
@@ -377,6 +377,12 @@
         todo += work(term, add_term, hop - 1)
         if whole_tiles and hop < hops:
             todo = work(own, add_own, hop + 1) + todo
+        if hop == hops:
+            drain(hops)
+            for stream in (low, own, tiles):
+                stream.finish()
+            for crossing in crossings:
+                crossing.wait_send()
         rounds = term.rounds(hop)
         share = -(-len(todo) // len(rounds))
         for arrivals in rounds:
@@ -400,11 +406,7 @@
             rows = [t * per_tile + part for part in range(per_tile)]
             out_ref[...] += product([t], own_all, rows)
 
-    drain(hops)
-    for stream in (low, own, term, tiles):
-        stream.finish()
-    for crossing in crossings:
-        crossing.wait_send()
+    term.finish()
 
 
 def local(

time: 46.9 us -> 46.9 us (level)
  no operation moved by 1% of the time
where the time goes in v6:
time: 46.9 us; the launch traced here: 46.8 us
  Pallas kernels  45.4 us (97%)
  local copies, waits for them, and re-layouts  0.71 us (2%)
  between operations  0.66 us (1%)
    pallas_call x1, Pallas kernels, local(): pl.pallas_call(functools.partial(kernel, count), out_shape=pltpu.VMEM((ow...  45.4 us

profile of v6, /device:TPU:0, one launch (start us, length us, event | category | flops | bytes accessed | tf_op | source)
XLA Modules:
  0.0 46.8 jit_solution(3575686722836973908)
XLA Ops:
  0.7 45.4 %shard_map.82 = f32[512,128]{1,0:T(8,128)S(1)} custom-call(f32[512,128]{1,0:T(8,128)} %guess_hbm.1, f32[512,128]{1,0:T(8,128)} %right_hbm.1, f32[1,512]{1,0:T(1,128)} %bitcast.3, bf16[512,8192]{1,0:T(8,128)(2,1)} %precon_hbm.1, bf16[1,256,768]{2,1,0:T(8,128)(2,1)} %border_hbm.1, bf16[1,256,512]{2,1,0:T(8,128)(2,1)} %inverse_hbm.1, s32[1,1]{1,0:T(1,128)} %bitcast.2.live_hbm, ...), custom_call_target="tpu_custom_call" | custom-call | tf_op jit(solution)/shard_map/pallas_call | solution.py:442
  46.1 0.7 %copy.10 = f32[512,128]{1,0:T(8,128)} copy(f32[512,128]{1,0:T(8,128)S(1)} %shard_map.82) | data formatting | bytes 524288
